TPU v7x, 1024 devices: a whole 4x4x32 slice. The times are simulated.
1024 devices in a mesh: group: 2 (over y_hi), row: 64 (over z, y_lo), col: 8 (over x, core).
Axes of the slice: x: 4, y: 4 (y_hi: 2, y_lo: 2; y = y_hi * 2 + y_lo), z: 32, core: 2. Of those that a mesh axis runs over, the one named last changes fastest.
Arguments:
- tokens: bfloat16 [4096, 5120], P('row', ('group', 'col')), may hold values from -6 to 6
- cotangent: bfloat16 [4096, 12800], P(('group', 'col'), 'row'), may hold values from -0.09375 to 0.09375
- master: float32 [12800, 5120], P('row', ('group', 'col')), may hold values from -0.078125 to 0.078125
- moment: float32 [12800, 5120], P('row', ('group', 'col')), may hold values from -6 to 6
- second: float32 [12800, 5120], P('row', ('group', 'col')), may hold values from 0.1 to 4
- prompts: bfloat16 [1024, 5120], P(('group', 'col')), may hold values from -6 to 6
- up_weight: bfloat16 [12800, 5120], P('row'), may hold values from -0.078125 to 0.078125
- down_weight: bfloat16 [12800, 5120], P('row'), may hold values from -0.0546875 to 0.0546875
Outputs:
- master_new: float32 [12800, 5120], P('row', ('group', 'col'))
- moment_new: float32 [12800, 5120], P('row', ('group', 'col'))
- second_new: float32 [12800, 5120], P('row', ('group', 'col'))
- prefill: float32 [1024, 5120], P(('group', 'col'), 'row')
All inputs are finite; a program needn't handle non-finite values.
Results may differ from a plain program's by a relative error of at most 0.0041.
Values may be sent and summed in bfloat16 or wider, within the bound.
A program may use at most 32 MiB of HBM per device.

v0:
```python
import jax
import jax.numpy as jnp
from jax import lax
from jax.sharding import Mesh
from jax.sharding import PartitionSpec as P

ROW = ("row_0", "row_1")


beta_first = 0.9
beta_second = 0.95
learn_rate = 0.002
weight_decay = 0.1
epsilon = 1e-08
first_bias = 1.0 - 0.9**10
second_bias = 1.0 - 0.95**10


def laid_out(pieces, dim):
    lengths = list(pieces.shape[1:])
    lengths[dim] *= pieces.shape[0]
    return jnp.moveaxis(pieces, 0, dim).reshape(lengths)


def from_everyone(x, axis):
    copies = jnp.broadcast_to(x, (lax.axis_size(axis), *x.shape))
    return lax.all_to_all(copies, axis, split_axis=0, concat_axis=0, tiled=True)


def collect(x, axis, dim):
    return laid_out(from_everyone(x, axis), dim)


def gather_axes(x, axes, dim):
    for axis in reversed(axes):
        x = lax.all_gather(x, axis, axis=dim, tiled=True)
    return x


def in_blocks(x, dim, length):
    lengths = x.shape
    pieces = x.reshape(*lengths[:dim], length, lengths[dim] // length, *lengths[dim + 1 :])
    return jnp.moveaxis(pieces, dim, 0)


def sum_at_owner(x, axis, dim):
    length = lax.axis_size(axis)
    pieces = lax.all_to_all(in_blocks(x, dim, length), axis, 0, 0, tiled=True)
    return jnp.sum(pieces, axis=0)


def own_rows(subtotal, axes):
    for axis in axes:
        subtotal = lax.psum_scatter(subtotal, axis, scatter_dimension=0, tiled=True)
    return subtotal


def adam_update(gradient, master, moment, second):
    moment_new = beta_first * moment + (1.0 - beta_first) * gradient
    second_new = beta_second * second + (1.0 - beta_second) * gradient * gradient
    direction = moment_new / first_bias / (jnp.sqrt(second_new / second_bias) + epsilon)
    master_new = master - learn_rate * (direction + weight_decay * master)
    return (master_new, moment_new, second_new)


def shards(tokens, cotangent, master, moment, second, prompts, up_weight, down_weight):
    cotangent_all = collect(cotangent, ("group", "col"), 0)
    window = cotangent_all
    gradient = jnp.einsum(
        "tf,td->fd", window, gather_axes(tokens, ROW, 0), preferred_element_type=jnp.float32
    )
    master_new, moment_new, second_new = adam_update(gradient, master, moment, second)
    refreshed = master_new.astype(jnp.bfloat16)
    prompt_cols = lax.all_to_all(prompts, ("group", "col"), split_axis=1, concat_axis=0, tiled=True)
    window = prompt_cols
    gate_pre = sum_at_owner(
        jnp.einsum("nd,fd->nf", window, refreshed, preferred_element_type=jnp.float32),
        ("group", "col"),
        0,
    )
    up_pre = jnp.einsum("nd,fd->nf", prompts, up_weight, preferred_element_type=jnp.float32)
    hidden = (jax.nn.silu(gate_pre) * up_pre).astype(jnp.bfloat16)
    window = down_weight
    prefill = own_rows(
        jnp.einsum("fd,nf->dn", window, hidden, preferred_element_type=jnp.float32), ROW
    ).T
    return (master_new, moment_new, second_new, prefill)


def solution(mesh):
    split = Mesh(
        mesh.devices.reshape(mesh.shape["group"], 32, 2, mesh.shape["col"]),
        ("group", "row_0", "row_1", "col"),
    )
    in_specs = (
        P(ROW, ("group", "col")),
        P(("group", "col"), ROW),
        P(ROW, ("group", "col")),
        P(ROW, ("group", "col")),
        P(ROW, ("group", "col")),
        P(("group", "col"), None),
        P(ROW, None),
        P(ROW, None),
    )
    out_specs = (
        P(ROW, ("group", "col")),
        P(ROW, ("group", "col")),
        P(ROW, ("group", "col")),
        P(("group", "col"), ROW),
    )
    return jax.shard_map(
        shards, mesh=split, in_specs=in_specs, out_specs=out_specs, check_vma=False
    )
```

profile of v0, /device:TPU:8, one launch (start us, length us, event | category | flops | bytes accessed | tf_op | source)
XLA Modules:
  0.0 366.7 jit_solution(4056048742399085334)
XLA Ops:
  7.2 0.0 copy-start
  7.2 0.0 all-gather.2.cloned.1.call-start
  7.2 17.7 %all_gather.6 = bf16[128,320]{1,0:T(8,128)(2,1)} all-gather(bf16[64,320]{1,0:T(8,128)(2,1)} %param.8), channel_id=1, replica_groups=mesh['group'=2,'row_0'=32,'row_1'=2,'col'=8] {'row_1'}, dimensions={0}, use_global_device_ids=true | all-gather | bytes 122880 | tf_op jit(solution)/shard_map/all_gather | solution.py:36
  24.9 0.0 all-gather.2.cloned.1.call-update
  24.9 2.2 broadcast_in_dim.3
  27.1 0.0 copy-start.1
  27.1 4.5 %all-to-all-start = ((bf16[16,256,200]{1,2,0:T(8,128)(2,1)}), bf16[16,256,200]{1,2,0:T(8,128)(2,1)}, u32[]{:S(2)}, u32[]{:S(2)}) async-start(bf16[16,256,200]{1,2,0:T(8,128)(2,1)} %broadcast_in_dim.3), calls=%async_computation | async-start | bytes 3276800 | tf_op jit(solution)/shard_map/all_to_all | solution.py:27
  31.7 0.0 copy-done.1
  31.7 0.6 all_to_all.21
  32.3 1.1 copy.19
  33.4 0.0 copy-start.3
  33.4 22.6 %all-to-all-done = bf16[16,256,200]{1,2,0:T(8,128)(2,1)} async-done(((bf16[16,256,200]{1,2,0:T(8,128)(2,1)}), bf16[16,256,200]{1,2,0:T(8,128)(2,1)}, u32[]{:S(2)}, u32[]{:S(2)}) %all-to-all-start) | async-done | bytes 1638432 | tf_op jit(solution)/shard_map/all_to_all | solution.py:27
  55.9 3.6 all-to-all-start.1
  59.6 0.0 reduce-scatter.7.cloned.1.call-start
  59.6 2.8 copy.25
  62.5 98.6 %all-gather.2.cloned.1.call-done = bf16[4096,320]{1,0:T(8,128)(2,1)} async-done(((bf16[128,320]{1,0:T(8,128)(2,1)}), bf16[4096,320]{1,0:T(8,128)(2,1)}) %all-gather.2.cloned.1.call-update) | async-done | bytes 2621456 | tf_op jit(solution)/shard_map/all_gather | solution.py:36
  161.1 0.0 copy-done.3
  161.1 4.5 %multiply_subtract_fusion = (f32[200,320]{1,0:T(8,128)S(1)}, f32[200,320]{1,0:T(8,128)}, f32[200,320]{1,0:T(8,128)}) fusion(f32[200,320]{1,0:T(8,128)S(1)} %copy-done.3, f32[200,320]{1,0:T(8,128)} %param.11, f32[200,320]{1,0:T(8,128)} %param.12, bf16[4096,200]{0,1:T(8,128)(2,1)} %bitcast.21, bf16[4096,320]{1,0:T(8,128)(2,1)} %all-gather.2.cloned.1.call-done), kind=kOutput, calls=%fused_computation.6 | convolution fusion | flops 525248000 | bytes 5795840 | tf_op jit(solution)/shard_map/tf,td->fd/dot_general | solution.py:69
  165.6 0.0 copy-start.2
  165.6 0.0 all-to-all-done.1
  165.6 0.7 copy-done.2
  166.3 1.3 convolution_bitcast_fusion.1
  167.7 1.5 copy.20
  169.1 24.0 %all_to_all.29 = f32[16,64,200]{2,1,0:T(8,128)} all-to-all(f32[16,64,200]{2,1,0:T(8,128)S(1)} %bitcast.19), channel_id=1, replica_groups=mesh['group'=2,'row_0'=32,'row_1'=2,'col'=8] {'group','col'}, dimensions={0} | all-to-all | bytes 1638400 | tf_op jit(solution)/shard_map/all_to_all | solution.py:48
  193.1 1.3 reduce_sum.9
  194.4 0.0 copy-done
  194.5 3.4 convolution_bitcast_fusion
  197.9 2.0 copy.21
  199.9 0.0 reduce-scatter.7.cloned.1.call-update
  199.9 0.0 reduce-scatter.9.cloned.1.call-start
  200.0 127.5 %reduce-scatter.7.cloned.1.call-done = f32[160,64]{1,0:T(8,128)} async-done(((f32[5120,64]{1,0:T(8,128)}), f32[160,64]{1,0:T(8,128)}) %reduce-scatter.7.cloned.1.call-update) | async-done | bytes 40976
  327.5 0.0 reduce-scatter.9.cloned.1.call-update
  327.5 31.2 %reduce-scatter.9.cloned.1.call-done = f32[80,64]{1,0:T(8,128)} async-done(((f32[160,64]{1,0:T(8,128)}), f32[80,64]{1,0:T(8,128)}) %reduce-scatter.9.cloned.1.call-update) | async-done | bytes 20496
  358.7 1.5 copy.24
Async XLA Ops:
  7.2 187.3 %copy-start = (bf16[200,5120]{1,0:T(8,128)(2,1)S(1)}, bf16[200,5120]{1,0:T(8,128)(2,1)}, u32[]{:S(2)}) copy-start(bf16[200,5120]{1,0:T(8,128)(2,1)} %param.15) | copy-start | bytes 6144004
  7.2 153.9 %all-gather.2.cloned.1.call-start = ((), (), s32[]{:S(2)}) async-start(), calls=%async_computation.5 | async-start | bytes 3244032 | tf_op jit(solution)/shard_map/all_gather | solution.py:36
  27.1 4.5 %copy-start.1 = (bf16[64,5120]{1,0:T(8,128)(2,1)S(1)}, bf16[64,5120]{1,0:T(8,128)(2,1)}, u32[]{:S(2)}) copy-start(bf16[64,5120]{1,0:T(8,128)(2,1)} %param.13) | copy-start | bytes 1966084
  27.1 28.8 %all-to-all-start = ((bf16[16,256,200]{1,2,0:T(8,128)(2,1)}), bf16[16,256,200]{1,2,0:T(8,128)(2,1)}, u32[]{:S(2)}, u32[]{:S(2)}) async-start(bf16[16,256,200]{1,2,0:T(8,128)(2,1)} %broadcast_in_dim.3), calls=%async_computation | async-start | bytes 3276800 | tf_op jit(solution)/shard_map/all_to_all | solution.py:27
  33.4 127.7 %copy-start.3 = (f32[200,320]{1,0:T(8,128)S(1)}, f32[200,320]{1,0:T(8,128)}, u32[]{:S(2)}) copy-start(f32[200,320]{1,0:T(8,128)} %param.10) | copy-start | bytes 768004
  55.9 109.6 %all-to-all-start.1 = ((bf16[64,16,320]{2,0,1:T(8,128)(2,1)}), bf16[64,16,320]{2,0,1:T(8,128)(2,1)S(1)}, u32[]{:S(2)}, u32[]{:S(2)}) async-start(bf16[64,16,320]{2,0,1:T(8,128)(2,1)} %copy.19), calls=%async_computation.1 | async-start | bytes 1572864 | tf_op jit(solution)/shard_map/all_to_all | solution.py:74
  59.6 267.9 %reduce-scatter.7.cloned.1.call-start = ((), (), s32[]{:S(2)}) async-start(), calls=%async_computation.6 | async-start | bytes 2703360
  165.6 0.7 copy-start.2
  199.9 158.8 %reduce-scatter.9.cloned.1.call-start = ((), (), s32[]{:S(2)}) async-start(), calls=%async_computation.7 | async-start | bytes 122880
Sparse Core Ops, SparseCore 0:
  25.0 136.0 all-gather.1
  200.0 127.3 reduce-scatter.6
  330.8 27.8 reduce-scatter.8
where the time goes:
time: 367 us
  waiting for transfers between devices  280 us (76%)
  blocking collectives  41.7 us (11%)
  between operations  13.8 us (4%)
  local copies, waits for them, and re-layouts  12.5 us (3%)
  matrix products  9.25 us (3%)
  starting transfers between devices  8.27 us (2%)
    unnamed x5, waiting for transfers between devices  159 us
    all_gather x1, waiting for transfers between devices, gather_axes(): x = lax.all_gather(x, axis, axis=dim, tiled=True)  98.6 us
    all_to_all x1, blocking collectives, sum_at_owner(): pieces = lax.all_to_all(in_blocks(x, dim, length), axis, 0, 0, tiled=True)  24 us
    all_to_all x1, waiting for transfers between devices, from_everyone(): return lax.all_to_all(copies, axis, split_axis=0, concat_axis=0, tiled=True)  22.6 us
    all_gather x1, blocking collectives, gather_axes(): x = lax.all_gather(x, axis, axis=dim, tiled=True)  17.7 us
  transfers between devices with their start and end apart: 5, of which 4 were waited for; matrix products, arithmetic and copies ran while one was open for 3% of the time, Pallas kernels for 0%

commit v1 on v0

v1 whole, which is shorter than its diff:
```python
import functools

import jax
import jax.numpy as jnp
from jax import lax
from jax.experimental import pallas as pl
from jax.experimental.pallas import tpu as pltpu
from jax.sharding import Mesh
from jax.sharding import PartitionSpec as P

AXES = ("yh", "z", "yl", "x", "core")
ROW = ("z", "yl")
GC = ("yh", "x", "core")
NZ = 32
MESH = pl.DeviceIdType.MESH
f32 = jnp.float32
bf16 = jnp.bfloat16

beta_first = 0.9
beta_second = 0.95
learn_rate = 0.002
weight_decay = 0.1
epsilon = 1e-08
first_bias = 1.0 - 0.9**10
second_bias = 1.0 - 0.95**10


def adam_update(gradient, master, moment, second):
    moment_new = beta_first * moment + (1.0 - beta_first) * gradient
    second_new = beta_second * second + (1.0 - beta_second) * gradient * gradient
    direction = moment_new / first_bias / (jnp.sqrt(second_new / second_bias) + epsilon)
    master_new = master - learn_rate * (direction + weight_decay * master)
    return (master_new, moment_new, second_new)


def wrap(v, n):
    return lax.rem(v + 4 * n, n)


def nt(a, b):
    return lax.dot_general(a, b, (((1,), (1,)), ((), ())), preferred_element_type=f32)


def nn(a, b):
    return jnp.dot(a, b, preferred_element_type=f32)


def kernel(
    tok_ref, cot_ref, master_hbm, moment_hbm, second_hbm, prompts_hbm, up_hbm, down_hbm,
    master_out, moment_out, second_out, prefill_out,
    master_v, moment_v, second_v, prompts_v, up_v, down_v, dperm,
    tsib, csib, tok_all, cs_send, cot_all, p_all,
    gsend, grecv, rsend, rrecv, rcat,
    gp32, gps, gpr, y32, ysend, yrecv, a32, asend, arecv, b32, bsend, brecv,
    loc_sem, d2d_s, d2d_r, js, jr, hs, hr, fs, fr,
    c1s, c1r, c2s, c2r, xs, xr, x2s, x2r, cfs, cfr,
    ps, pr, gs, gr, ys, yr, as_, ar, bs, br,
):
    yh, z, yl, x, c = (lax.axis_index(a) for a in AXES)
    h = yh * 4 + x
    zh, zl = z // 4, lax.rem(z, 4)
    sib = {"core": 1 - c}
    yn = {"yl": 1 - yl}
    sends = []

    def remote(src, dst, ssem, rsem, peer):
        return pltpu.make_async_remote_copy(
            src_ref=src, dst_ref=dst, send_sem=ssem, recv_sem=rsem,
            device_id=peer, device_id_type=MESH,
        )

    loads = []
    for n, (a, b) in enumerate(
        ((prompts_hbm, prompts_v), (master_hbm, master_v), (moment_hbm, moment_v),
         (second_hbm, second_v), (down_hbm, down_v), (up_hbm, up_v))
    ):
        cp = pltpu.make_async_copy(a, b, loc_sem.at[n])
        cp.start()
        loads.append(cp)

    def chip_peer(k):
        o = lax.rem(h + k, 8)
        return o, {"yh": o // 4, "x": lax.rem(o, 4)}

    def near_peer(k):
        o = lax.rem(zl + k, 4)
        return o, {"z": zh * 4 + o}

    barrier = pltpu.get_barrier_semaphore()
    peers = [sib, yn]
    peers += [{"z": wrap(z + d, NZ)} for d in (1, -1, 2, -2)]
    peers += [near_peer(k)[1] for k in range(1, 4)]
    peers += [chip_peer(k)[1] for k in range(1, 8)]
    for peer in peers:
        pl.semaphore_signal(barrier, inc=1, device_id=peer, device_id_type=MESH)
    pl.semaphore_wait(barrier, len(peers))

    tok_d2d = remote(tok_ref, tsib, d2d_s.at[0], d2d_r.at[0], sib)
    cot_d2d = remote(cot_ref, csib, d2d_s.at[0], d2d_r.at[0], sib)

    def block(d):
        return wrap(z - d, NZ)

    order = {0: 0}
    for d in range(1, 16):
        order[d] = len(order)
        order[-d] = len(order)
    order[16] = len(order)

    def fwd(d):
        b = tok_all.at[block(d)]
        return remote(b, b, fs.at[order[d]], fr.at[order[d]], sib)

    def jump(dr, k):
        b = tok_all.at[block(dr * 2 * k)]
        i = 0 if dr > 0 else 1
        return remote(b, b, js.at[i, k], jr.at[i, k], {"z": wrap(z + 2 * dr, NZ)})

    def jump_in(dr, k):
        b = tok_all.at[block(dr * 2 * (k + 1))]
        i = 0 if dr > 0 else 1
        return remote(b, b, js.at[i, k], jr.at[i, k], {"z": wrap(z + 2 * dr, NZ)})

    def hop(dr, k):
        b = tok_all.at[block(dr * 2 * k)]
        i = 0 if dr > 0 else 1
        return remote(b, b, hs.at[i, k], hr.at[i, k], {"z": wrap(z + dr, NZ)})

    def hop_in(dr, k):
        b = tok_all.at[block(dr * (2 * k + 1))]
        i = 0 if dr > 0 else 1
        return remote(b, b, hs.at[i, k], hr.at[i, k], {"z": wrap(z + dr, NZ)})

    def njump(dr):
        return 8 if dr > 0 else 7

    def prompt_send(k):
        o, peer = chip_peer(k)
        return remote(
            prompts_v.at[:, pl.ds(pl.multiple_of(o * 640, 128), 640)],
            p_all.at[h], ps.at[k], pr.at[k], peer,
        )

    def send_prompts():
        loads[0].wait()
        for k in range(1, 8):
            prompt_send(k).start()
        p_all[h] = prompts_v[:, pl.ds(pl.multiple_of(h * 640, 128), 640)]

    hy = (1 - yh) * 4 + x

    def hx(sel, d):
        return (yh if sel == 0 else 1 - yh) * 4 + wrap(x + d, 4)

    cot1 = remote(cs_send, cot_all.at[h, yl], c1s, c1r, yn)
    cot1_in = remote(cs_send, cot_all.at[h, 1 - yl], c1s, c1r, yn)
    cot2 = remote(cot_all.at[h], cot_all.at[h], c2s, c2r, {"yh": 1 - yh})
    cot2_in = remote(cot_all.at[hy], cot_all.at[hy], c2s, c2r, {"yh": 1 - yh})

    def xsend(sel, dr):
        b = cot_all.at[hx(sel, 0)]
        i = 0 if dr > 0 else 1
        return remote(b, b, xs.at[i, sel], xr.at[i, sel], {"x": wrap(x + dr, 4)})

    def xin(sel, dr):
        b = cot_all.at[hx(sel, -dr)]
        i = 0 if dr > 0 else 1
        return remote(b, b, xs.at[i, sel], xr.at[i, sel], {"x": wrap(x + dr, 4)})

    def x2send(sel, dr):
        i = 0 if dr > 0 else 1
        b = cot_all.at[hx(sel, -dr), i]
        return remote(b, b, x2s.at[i, sel], x2r.at[i, sel], {"x": wrap(x + dr, 4)})

    def x2in(sel, dr):
        i = 0 if dr > 0 else 1
        b = cot_all.at[hx(sel, -2 * dr), i]
        return remote(b, b, x2s.at[i, sel], x2r.at[i, sel], {"x": wrap(x + dr, 4)})

    def cfwd(n):
        if n == 0:
            b = cot_all.at[h]
        elif n == 1:
            b = cot_all.at[hy]
        elif n < 6:
            sel, i = (n - 2) // 2, (n - 2) % 2
            b = cot_all.at[hx(sel, -1 if i == 0 else 1)]
        else:
            sel, i = (n - 6) // 2, (n - 6) % 2
            b = cot_all.at[hx(sel, 2), i]
        return remote(b, b, cfs.at[n], cfr.at[n], sib)

    @pl.when(c == 1)
    def _():
        cot_d2d.start()
        tok_d2d.wait_recv()
        mine, other = tok_ref[...], tsib[...]
        tok_all[z] = jnp.concatenate(
            [other[:, :256], mine[:, :256], other[:, 256:], mine[:, 256:]], axis=1
        )
        for dr in (1, -1):
            jump(dr, 0).start()
            hop(dr, 0).start()
        fwd(0).start()
        for k in range(1, 9):
            for dr in (1, -1):
                if k <= njump(dr):
                    jump_in(dr, k - 1).wait_recv()
                    if k < njump(dr):
                        jump(dr, k).start()
                    if k < 8:
                        hop(dr, k).start()
                    fwd(dr * 2 * k).start()
            for dr in (1, -1):
                hop_in(dr, k - 1).wait_recv()
                fwd(dr * (2 * k - 1)).start()
            if k == 2:
                send_prompts()
        for n in range(10):
            cfwd(n).wait_recv()

    @pl.when(c == 0)
    def _():
        tok_d2d.start()
        cot_d2d.wait_recv()
        for core, src in ((0, cot_ref), (1, csib)):
            v = src[...]
            even = jnp.concatenate([v[:, :64], v[:, 128:192]], axis=1)
            odd = jnp.concatenate([v[:, 64:128], v[:, 192:]], axis=1)
            first = yl == 0
            cot_all[h, yl, core] = jnp.where(first, even, odd)
            cs_send[core] = jnp.where(first, odd, even)
        cot1.start()
        cot1_in.wait_recv()
        cot2.start()
        for dr in (1, -1):
            xsend(0, dr).start()
        cfwd(0).start()
        cot2_in.wait_recv()
        for dr in (1, -1):
            xsend(1, dr).start()
        cfwd(1).start()
        for sel in range(2):
            for i, dr in enumerate((1, -1)):
                xin(sel, dr).wait_recv()
                x2send(sel, dr).start()
                cfwd(2 + 2 * sel + i).start()
        send_prompts()
        for sel in range(2):
            for i, dr in enumerate((1, -1)):
                x2in(sel, dr).wait_recv()
                cfwd(6 + 2 * sel + i).start()
        for d in order:
            fwd(d).wait_recv()

    first_core = c == 0

    def gradient(part):
        wide = jnp.zeros((200, 256), f32)
        rest = jnp.zeros((200, 128), f32)
        for o in range(8):
            lhs = jnp.concatenate([cot_all[o, part, 0], cot_all[o, part, 1]], axis=1)
            t = tok_all[4 * o : 4 * o + 4, :, pl.ds(pl.multiple_of(c * 256, 256), 256)]
            wide += nn(lhs, t.reshape(256, 256))
            rest += nn(lhs, tok_all[4 * o : 4 * o + 4, :, 512:640].reshape(256, 128))
        return wide, jnp.where(first_core, rest[:, :64], rest[:, 64:])

    wide, rest = gradient(1 - yl)
    gsend[:, :256] = wide.astype(bf16)
    gsend[:, 256:] = rest.astype(bf16)
    gcp = remote(gsend, grecv, d2d_s.at[1], d2d_r.at[1], yn)
    gcp.start()
    wide, rest = gradient(yl)
    for n in (1, 2, 3, 4):
        loads[n].wait()
    for r in range(64):
        zz, l = r // 2, r % 2
        at = ((l * 4 + zz % 4) * 8 + zz // 4) * 80
        dperm[:, at : at + 80] = down_v[:, 80 * r : 80 * r + 80]
    gcp.wait_recv()
    for part, lanes in ((wide, slice(0, 256)), (rest, slice(256, 320))):
        total = part + grecv[:, lanes].astype(f32)
        new = adam_update(total, master_v[:, lanes], moment_v[:, lanes], second_v[:, lanes])
        master_out[:, lanes] = new[0]
        moment_out[:, lanes] = new[1]
        second_out[:, lanes] = new[2]
        rsend[:, lanes] = new[0].astype(bf16)
    rcp = remote(rsend, rrecv, d2d_s.at[2], d2d_r.at[2], sib)
    rcp.start()
    for k in range(1, 8):
        prompt_send(k).wait_recv()
    rcp.wait_recv()
    mine, other = rsend[...], rrecv[...]
    rcat[:, :320] = jnp.where(first_core, mine, other)
    rcat[:, 320:] = jnp.where(first_core, other, mine)

    for o in range(8):
        v = nt(p_all[o], rcat[...])
        gp32[o] = v
        gps[o] = v.astype(bf16)

    def gate_send(k):
        o, peer = chip_peer(k)
        return remote(gps.at[o], gpr.at[h], gs.at[k], gr.at[k], peer)

    for k in (4, 2, 6, 1, 3, 5, 7):
        gate_send(k).start()
    loads[5].wait()
    up_pre = nt(prompts_v[...], up_v[...])
    gate = gp32[h]
    for k in range(1, 8):
        gate_send(k).wait_recv()
        gate += gpr[wrap(h - k, 8)].astype(f32)
    hidden = (gate / (1.0 + jnp.exp(-gate)) * up_pre).astype(bf16)

    def half(l):
        return dperm[:, pl.ds(pl.multiple_of(l * 2560, 128), 2560)]

    ysend[...] = nn(hidden, half(1 - yl)).astype(bf16)
    ycp = remote(ysend, yrecv, ys, yr, yn)
    ycp.start()
    y32[...] = nn(hidden, half(yl))
    ycp.wait_recv()
    for o in range(4):
        v = y32[:, 640 * o : 640 * o + 640] + yrecv[:, 640 * o : 640 * o + 640].astype(f32)
        a32[o] = v
        asend[o] = v.astype(bf16)

    def near_send(k):
        o, peer = near_peer(k)
        return remote(asend.at[o], arecv.at[zl], as_.at[k], ar.at[k], peer)

    for k in range(1, 4):
        near_send(k).start()
    total = a32[zl]
    for k in range(1, 4):
        near_send(k).wait_recv()
        total += arecv[wrap(zl - k, 4)].astype(f32)
    for o in range(8):
        v = total[:, 80 * o : 80 * o + 80]
        b32[o] = v
        bsend[o] = v.astype(bf16)

    def far_send(k):
        o = lax.rem(zh + k, 8)
        return remote(bsend.at[o], brecv.at[zh], bs.at[k], br.at[k], {"z": o * 4 + zl})

    for k in (4, 3, 5, 2, 6, 1, 7):
        far_send(k).start()
    total = b32[zh]
    for k in (1, 7, 2, 6, 3, 5, 4):
        far_send(k).wait_recv()
        total += brecv[wrap(zh - k, 8)].astype(f32)
    prefill_out[...] = total

    @pl.when(c == 1)
    def _():
        cot_d2d.wait_send()
        for dr in (1, -1):
            for k in range(8):
                if k < njump(dr):
                    jump(dr, k).wait_send()
                hop(dr, k).wait_send()
        for d in order:
            fwd(d).wait_send()

    @pl.when(c == 0)
    def _():
        tok_d2d.wait_send()
        cot1.wait_send()
        cot2.wait_send()
        for sel in range(2):
            for dr in (1, -1):
                xsend(sel, dr).wait_send()
                x2send(sel, dr).wait_send()
        for n in range(10):
            cfwd(n).wait_send()

    for cp in (gcp, rcp, ycp):
        cp.wait_send()
    for k in range(1, 8):
        prompt_send(k).wait_send()
        gate_send(k).wait_send()
        far_send(k).wait_send()
    for k in range(1, 4):
        near_send(k).wait_send()


def shards(tokens, cotangent, master, moment, second, prompts, up_weight, down_weight):
    V, D = pltpu.VMEM, pltpu.SemaphoreType.DMA
    vmem = pl.BlockSpec(memory_space=pltpu.VMEM)
    hbm = pl.BlockSpec(memory_space=pl.ANY)
    out = jax.ShapeDtypeStruct
    return pl.pallas_call(
        kernel,
        out_shape=(
            out((200, 320), f32), out((200, 320), f32), out((200, 320), f32), out((64, 80), f32),
        ),
        in_specs=[vmem] * 2 + [hbm] * 6,
        out_specs=[vmem] * 4,
        scratch_shapes=[
            V((200, 320), f32), V((200, 320), f32), V((200, 320), f32),
            V((64, 5120), bf16), V((200, 5120), bf16), V((200, 5120), bf16), V((200, 5120), bf16),
            V((64, 320), bf16), V((200, 256), bf16), V((32, 64, 640), bf16),
            V((2, 200, 128), bf16), V((8, 2, 2, 200, 128), bf16), V((8, 64, 640), bf16),
            V((200, 320), bf16), V((200, 320), bf16), V((200, 320), bf16), V((200, 320), bf16),
            V((200, 640), bf16),
            V((8, 64, 200), f32), V((8, 64, 200), bf16), V((8, 64, 200), bf16),
            V((64, 2560), f32), V((64, 2560), bf16), V((64, 2560), bf16),
            V((4, 64, 640), f32), V((4, 64, 640), bf16), V((4, 64, 640), bf16),
            V((8, 64, 80), f32), V((8, 64, 80), bf16), V((8, 64, 80), bf16),
            D((6,)), D((3,)), D((3,)), D((2, 8)), D((2, 8)), D((2, 8)), D((2, 8)),
            D((32,)), D((32,)),
            D(()), D(()), D(()), D(()), D((2, 2)), D((2, 2)), D((2, 2)), D((2, 2)),
            D((10,)), D((10,)),
            D((8,)), D((8,)), D((8,)), D((8,)), D(()), D(()), D((4,)), D((4,)), D((8,)), D((8,)),
        ],
        compiler_params=pltpu.CompilerParams(
            collective_id=0, has_side_effects=True, vmem_limit_bytes=56 * 1024 * 1024
        ),
    )(tokens, cotangent.T, master, moment, second, prompts, up_weight, down_weight)


def solution(mesh):
    split = Mesh(mesh.devices.reshape(2, NZ, 2, 4, 2), AXES)
    tile, rows = P(ROW, GC), P(GC, ROW)
    return jax.shard_map(
        shards,
        mesh=split,
        in_specs=(tile, rows, tile, tile, tile, P(GC, None), P(ROW, None), P(ROW, None)),
        out_specs=(tile, tile, tile, rows),
        check_vma=False,
    )
```

time: 367 us -> 114 us (0.31)
  the two profiles are of different devices: /device:TPU:8 before, /device:TPU:110 now
where the time goes in v1:
time: 114 us
  Pallas kernels  107 us (94%)
  local copies, waits for them, and re-layouts  6.48 us (6%)
    pallas_call x1, Pallas kernels, shards(): pl.pallas_call(kernel, out_shape=(out((200, 320), f32), out((200, 320), f...  107 us
    unnamed x4, local copies, waits for them, and re-layouts  6.48 us

profile of v1, /device:TPU:110, one launch (start us, length us, event | category | flops | bytes accessed | tf_op | source)
XLA Modules:
  0.0 113.9 jit_solution(6327691503376029113)
XLA Ops:
  0.6 106.8 %shard_map.111 = (f32[200,320]{1,0:T(8,128)}, f32[200,320]{1,0:T(8,128)}, f32[200,320]{1,0:T(8,128)}, f32[64,80]{1,0:T(8,128)}) custom-call(bf16[64,320]{1,0:T(8,128)(2,1)} %tok_ref.1, bf16[200,256]{1,0:T(8,128)(2,1)} %bitcast.1, f32[200,320]{1,0:T(8,128)} %master_hbm.1, f32[200,320]{1,0:T(8,128)} %moment_hbm.1, f32[200,320]{1,0:T(8,128)} %second_hbm.1, ...), custom_call_target="tpu_custom_call" | custom-call | tf_op jit(solution)/shard_map/pallas_call | solution.py:394
  107.4 1.7 %copy.16 = f32[200,320]{1,0:T(8,128)} copy(f32[200,320]{1,0:T(8,128)} %get-tuple-element.8) | data formatting | bytes 512000
  109.1 1.7 %copy.17 = f32[200,320]{1,0:T(8,128)} copy(f32[200,320]{1,0:T(8,128)} %get-tuple-element.9) | data formatting | bytes 512000
  110.8 1.7 %copy.18 = f32[200,320]{1,0:T(8,128)} copy(f32[200,320]{1,0:T(8,128)} %get-tuple-element.10) | data formatting | bytes 512000
  112.5 1.4 %copy.19 = f32[64,80]{1,0:T(8,128)} copy(f32[64,80]{1,0:T(8,128)} %get-tuple-element.11) | data formatting | bytes 40960

commit v2 on v1

--- a/solution.py
+++ b/solution.py
@@ -12,6 +12,8 @@
 ROW = ("z", "yl")
 GC = ("yh", "x", "core")
 NZ = 32
+JUMP = 2
+CH = 4
 MESH = pl.DeviceIdType.MESH
 f32 = jnp.float32
 bf16 = jnp.bfloat16
@@ -46,15 +48,16 @@
 
 
 def kernel(
-    tok_ref, cot_ref, master_hbm, moment_hbm, second_hbm, prompts_hbm, up_hbm, down_hbm,
-    master_out, moment_out, second_out, prefill_out,
-    master_v, moment_v, second_v, prompts_v, up_v, down_v, dperm,
+    tok_hbm, cot_hbm, master_hbm, moment_hbm, second_hbm, prompts_hbm, up_hbm, down_hbm,
+    master_hout, moment_hout, second_hout, prefill_out,
+    master_out, moment_out, second_out,
+    tok_ref, cot_ref, master_v, moment_v, second_v, prompts_v, up_v, down_v, dperm, dother,
     tsib, csib, tok_all, cs_send, cot_all, p_all,
     gsend, grecv, rsend, rrecv, rcat,
-    gp32, gps, gpr, y32, ysend, yrecv, a32, asend, arecv, b32, bsend, brecv,
-    loc_sem, d2d_s, d2d_r, js, jr, hs, hr, fs, fr,
+    gp32, gps, gpr, hid, hrecv, a32, asend, arecv, b32, bsend, brecv,
+    loc_sem, st_sem, d2d_s, d2d_r, js, jr, hs, hr, fs, fr,
     c1s, c1r, c2s, c2r, xs, xr, x2s, x2r, cfs, cfr,
-    ps, pr, gs, gr, ys, yr, as_, ar, bs, br,
+    ps, pr, gs, gr, ds_, dr_, as_, ar, bs, br,
 ):
     yh, z, yl, x, c = (lax.axis_index(a) for a in AXES)
     h = yh * 4 + x
@@ -72,28 +75,38 @@
     loads = []
     for n, (a, b) in enumerate(
         ((prompts_hbm, prompts_v), (master_hbm, master_v), (moment_hbm, moment_v),
-         (second_hbm, second_v), (down_hbm, down_v), (up_hbm, up_v))
+         (second_hbm, second_v), (down_hbm, down_v), (up_hbm, up_v),
+         (tok_hbm, tok_ref), (cot_hbm, cot_ref))
     ):
         cp = pltpu.make_async_copy(a, b, loc_sem.at[n])
-        cp.start()
         loads.append(cp)
+    for n in (6, 7, 0, 4, 1, 2, 3, 5):
+        loads[n].start()
 
     def chip_peer(k):
         o = lax.rem(h + k, 8)
         return o, {"yh": o // 4, "x": lax.rem(o, 4)}
 
-    def near_peer(k):
-        o = lax.rem(zl + k, 4)
-        return o, {"z": zh * 4 + o}
+    def prompt_peer(k):
+        o = lax.rem(h + k, 8)
+        return o, {"yh": o // 4, "x": lax.rem(o, 4), "yl": lax.rem(yl + yh + o // 4, 2)}
+
+    def near_peer(s, k):
+        u = wrap(z + 2 * s, NZ)
+        to = wrap(u // 4 * 4 + lax.rem(u + k, 4) - 2 * s, NZ)
+        return lax.rem(to, 4), {"z": to}
 
     barrier = pltpu.get_barrier_semaphore()
     peers = [sib, yn]
     peers += [{"z": wrap(z + d, NZ)} for d in (1, -1, 2, -2)]
-    peers += [near_peer(k)[1] for k in range(1, 4)]
+    peers += [near_peer(s, k)[1] for s in range(2) for k in range(1, 4)]
     peers += [chip_peer(k)[1] for k in range(1, 8)]
+    peers += [prompt_peer(k)[1] for k in range(1, 8)]
     for peer in peers:
         pl.semaphore_signal(barrier, inc=1, device_id=peer, device_id_type=MESH)
     pl.semaphore_wait(barrier, len(peers))
+    loads[6].wait()
+    loads[7].wait()
 
     tok_d2d = remote(tok_ref, tsib, d2d_s.at[0], d2d_r.at[0], sib)
     cot_d2d = remote(cot_ref, csib, d2d_s.at[0], d2d_r.at[0], sib)
@@ -111,31 +124,44 @@
         b = tok_all.at[block(d)]
         return remote(b, b, fs.at[order[d]], fr.at[order[d]], sib)
 
-    def jump(dr, k):
-        b = tok_all.at[block(dr * 2 * k)]
-        i = 0 if dr > 0 else 1
-        return remote(b, b, js.at[i, k], jr.at[i, k], {"z": wrap(z + 2 * dr, NZ)})
-
-    def jump_in(dr, k):
-        b = tok_all.at[block(dr * 2 * (k + 1))]
-        i = 0 if dr > 0 else 1
-        return remote(b, b, js.at[i, k], jr.at[i, k], {"z": wrap(z + 2 * dr, NZ)})
-
-    def hop(dr, k):
-        b = tok_all.at[block(dr * 2 * k)]
-        i = 0 if dr > 0 else 1
+    rows = 64 // CH
+    steps = 16 // JUMP
+
+    def side(dr):
+        return 0 if dr > 0 else 1
+
+    def piece(d, ch):
+        return tok_all.at[block(d), pl.ds(rows * ch, rows)]
+
+    def jump(dr, k, ch):
+        b, i = piece(dr * JUMP * k, ch), side(dr)
+        return remote(b, b, js.at[i, k], jr.at[i, k, ch], {"z": wrap(z + JUMP * dr, NZ)})
+
+    def jump_in(dr, k, ch):
+        b, i = piece(dr * JUMP * (k + 1), ch), side(dr)
+        return remote(b, b, js.at[i, k], jr.at[i, k, ch], {"z": wrap(z + JUMP * dr, NZ)})
+
+    def jump_out(dr, k):
+        b, i = tok_all.at[block(dr * JUMP * k)], side(dr)
+        return remote(b, b, js.at[i, k], jr.at[i, k, 0], {"z": wrap(z + JUMP * dr, NZ)})
+
+    def hop(dr, k, ch):
+        b, i = piece(dr * 2 * k, ch), side(dr)
         return remote(b, b, hs.at[i, k], hr.at[i, k], {"z": wrap(z + dr, NZ)})
 
+    def hop_out(dr, k):
+        b, i = tok_all.at[block(dr * 2 * k)], side(dr)
+        return remote(b, b, hs.at[i, k], hr.at[i, k], {"z": wrap(z + dr, NZ)})
+
     def hop_in(dr, k):
-        b = tok_all.at[block(dr * (2 * k + 1))]
-        i = 0 if dr > 0 else 1
+        b, i = tok_all.at[block(dr * (2 * k + 1))], side(dr)
         return remote(b, b, hs.at[i, k], hr.at[i, k], {"z": wrap(z + dr, NZ)})
 
     def njump(dr):
-        return 8 if dr > 0 else 7
+        return steps if dr > 0 else steps - 1
 
     def prompt_send(k):
-        o, peer = chip_peer(k)
+        o, peer = prompt_peer(k)
         return remote(
             prompts_v.at[:, pl.ds(pl.multiple_of(o * 640, 128), 640)],
             p_all.at[h], ps.at[k], pr.at[k], peer,
@@ -190,6 +216,10 @@
             b = cot_all.at[hx(sel, 2), i]
         return remote(b, b, cfs.at[n], cfr.at[n], sib)
 
+    down_y = remote(dperm.at[1 - yl], dother, ds_.at[0], dr_.at[0], yn)
+    down_own = remote(dperm.at[yl], dperm.at[yl], ds_.at[1], dr_.at[1], sib)
+    down_sib = remote(dother, dother, ds_.at[2], dr_.at[2], sib)
+
     @pl.when(c == 1)
     def _():
         cot_d2d.start()
@@ -198,23 +228,29 @@
         tok_all[z] = jnp.concatenate(
             [other[:, :256], mine[:, :256], other[:, 256:], mine[:, 256:]], axis=1
         )
-        for dr in (1, -1):
-            jump(dr, 0).start()
-            hop(dr, 0).start()
+        for ch in range(CH):
+            for dr in (1, -1):
+                jump(dr, 0, ch).start()
+                if JUMP == 2:
+                    hop(dr, 0, ch).start()
         fwd(0).start()
-        for k in range(1, 9):
-            for dr in (1, -1):
-                if k <= njump(dr):
-                    jump_in(dr, k - 1).wait_recv()
+        for k in range(1, steps + 1):
+            for ch in range(CH):
+                for dr in (1, -1):
+                    if k > njump(dr):
+                        continue
+                    jump_in(dr, k - 1, ch).wait_recv()
                     if k < njump(dr):
-                        jump(dr, k).start()
-                    if k < 8:
-                        hop(dr, k).start()
-                    fwd(dr * 2 * k).start()
-            for dr in (1, -1):
-                hop_in(dr, k - 1).wait_recv()
-                fwd(dr * (2 * k - 1)).start()
-            if k == 2:
+                        jump(dr, k, ch).start()
+                    if JUMP == 2 and k < steps:
+                        hop(dr, k, ch).start()
+                    if ch == CH - 1:
+                        fwd(dr * JUMP * k).start()
+            if JUMP == 2:
+                for dr in (1, -1):
+                    hop_in(dr, k - 1).wait_recv()
+                    fwd(dr * (2 * k - 1)).start()
+            if k == steps // 4:
                 send_prompts()
         for n in range(10):
             cfwd(n).wait_recv()
@@ -250,6 +286,15 @@
             for i, dr in enumerate((1, -1)):
                 x2in(sel, dr).wait_recv()
                 cfwd(6 + 2 * sel + i).start()
+        loads[4].wait()
+        for r in range(64):
+            zz, l = r // 2, r % 2
+            at, part = zz % 4 * 640, zz // 4
+            dperm[l, :, at + 64 * part : at + 64 * part + 64] = down_v[:, 80 * r : 80 * r + 64]
+            at += 512 + 16 * part
+            dperm[l, :, at : at + 16] = down_v[:, 80 * r + 64 : 80 * r + 80]
+        down_y.start()
+        down_own.start()
         for d in order:
             fwd(d).wait_recv()
 
@@ -271,12 +316,8 @@
     gcp = remote(gsend, grecv, d2d_s.at[1], d2d_r.at[1], yn)
     gcp.start()
     wide, rest = gradient(yl)
-    for n in (1, 2, 3, 4):
+    for n in (1, 2, 3):
         loads[n].wait()
-    for r in range(64):
-        zz, l = r // 2, r % 2
-        at = ((l * 4 + zz % 4) * 8 + zz // 4) * 80
-        dperm[:, at : at + 80] = down_v[:, 80 * r : 80 * r + 80]
     gcp.wait_recv()
     for part, lanes in ((wide, slice(0, 256)), (rest, slice(256, 320))):
         total = part + grecv[:, lanes].astype(f32)
@@ -285,8 +326,21 @@
         moment_out[:, lanes] = new[1]
         second_out[:, lanes] = new[2]
         rsend[:, lanes] = new[0].astype(bf16)
+    stores = []
+    for n, (a, b) in enumerate(
+        ((master_out, master_hout), (moment_out, moment_hout), (second_out, second_hout))
+    ):
+        stores.append(pltpu.make_async_copy(a, b, st_sem.at[n]))
     rcp = remote(rsend, rrecv, d2d_s.at[2], d2d_r.at[2], sib)
     rcp.start()
+    for cp in stores:
+        cp.start()
+
+    @pl.when(c == 0)
+    def _():
+        down_y.wait_recv()
+        down_sib.start()
+
     for k in range(1, 8):
         prompt_send(k).wait_recv()
     rcp.wait_recv()
@@ -312,61 +366,90 @@
         gate_send(k).wait_recv()
         gate += gpr[wrap(h - k, 8)].astype(f32)
     hidden = (gate / (1.0 + jnp.exp(-gate)) * up_pre).astype(bf16)
-
-    def half(l):
-        return dperm[:, pl.ds(pl.multiple_of(l * 2560, 128), 2560)]
-
-    ysend[...] = nn(hidden, half(1 - yl)).astype(bf16)
-    ycp = remote(ysend, yrecv, ys, yr, yn)
-    ycp.start()
-    y32[...] = nn(hidden, half(yl))
-    ycp.wait_recv()
+    hid[...] = hidden
+    hcp = remote(hid, hrecv, d2d_s.at[3], d2d_r.at[3], yn)
+    hcp.start()
+
+    @pl.when(c == 1)
+    def _():
+        down_own.wait_recv()
+        down_sib.wait_recv()
+
     for o in range(4):
-        v = y32[:, 640 * o : 640 * o + 640] + yrecv[:, 640 * o : 640 * o + 640].astype(f32)
+        a32[o] = nn(hidden, dperm[yl, :, 640 * o : 640 * o + 640])
+    hcp.wait_recv()
+    hidden = hrecv[...]
+
+    def near_send(s, k):
+        o, peer = near_peer(s, k)
+        part = pl.ds(32 * s, 32)
+        return remote(asend.at[o, part], arecv.at[k - 1, part], as_.at[s, k], ar.at[s, k], peer)
+
+    for o in range(4):
+        v = a32[o] + nn(hidden, dother[:, 640 * o : 640 * o + 640])
         a32[o] = v
         asend[o] = v.astype(bf16)
-
-    def near_send(k):
-        o, peer = near_peer(k)
-        return remote(asend.at[o], arecv.at[zl], as_.at[k], ar.at[k], peer)
-
-    for k in range(1, 4):
-        near_send(k).start()
-    total = a32[zl]
-    for k in range(1, 4):
-        near_send(k).wait_recv()
-        total += arecv[wrap(zl - k, 4)].astype(f32)
-    for o in range(8):
-        v = total[:, 80 * o : 80 * o + 80]
-        b32[o] = v
-        bsend[o] = v.astype(bf16)
+    for s in range(2):
+        for k in (2, 1, 3):
+            near_send(s, k).start()
 
     def far_send(k):
         o = lax.rem(zh + k, 8)
-        return remote(bsend.at[o], brecv.at[zh], bs.at[k], br.at[k], {"z": o * 4 + zl})
-
+        return remote(bsend.at[o], brecv.at[k - 1], bs.at[k], br.at[k], {"z": o * 4 + zl})
+
+    for s in range(2):
+        part = slice(32 * s, 32 * s + 32)
+        total = a32[zl, part]
+        for k in range(1, 4):
+            near_send(s, k).wait_recv()
+            total += arecv[k - 1, part].astype(f32)
+        a32[zl, part] = total
+    lane = lax.broadcasted_iota(jnp.int32, (32, 128), 1)
+    for o in range(4):
+        top = a32[zl, :32, 128 * o : 128 * o + 128]
+        low = a32[zl, 32:, 128 * o : 128 * o + 128]
+        even = jnp.where(lane < 64, top, pltpu.roll(low, 64, 1))
+        odd = jnp.where(lane < 64, pltpu.roll(top, 64, 1), low)
+        b32[2 * o, :32], b32[2 * o + 1, :32] = even, odd
+        bsend[2 * o, :32], bsend[2 * o + 1, :32] = even.astype(bf16), odd.astype(bf16)
+    last = a32[zl, :, 512:640]
+    rolled = [last] + [pltpu.roll(last, 16 * n, 1) for n in range(1, 8)]
+    sixteen = lax.broadcasted_iota(jnp.int32, (8, 128), 1) // 16
+    for o in range(8):
+        v = rolled[-o % 8][:8]
+        for q in range(1, 8):
+            v = jnp.where(sixteen == q, rolled[(q - o) % 8][8 * q : 8 * q + 8], v)
+        b32[o, 32:] = v
+        bsend[o, 32:] = v.astype(bf16)
     for k in (4, 3, 5, 2, 6, 1, 7):
         far_send(k).start()
     total = b32[zh]
     for k in (1, 7, 2, 6, 3, 5, 4):
         far_send(k).wait_recv()
-        total += brecv[wrap(zh - k, 8)].astype(f32)
-    prefill_out[...] = total
+        total += brecv[k - 1].astype(f32)
+    prefill_out[:32, :64] = total[:32, :64]
+    prefill_out[32:, :64] = total[:32, 64:]
+    for q in range(8):
+        prefill_out[8 * q : 8 * q + 8, 64:] = total[32:, 16 * q : 16 * q + 16]
 
     @pl.when(c == 1)
     def _():
         cot_d2d.wait_send()
         for dr in (1, -1):
-            for k in range(8):
+            for k in range(steps):
                 if k < njump(dr):
-                    jump(dr, k).wait_send()
-                hop(dr, k).wait_send()
+                    jump_out(dr, k).wait_send()
+                if JUMP == 2:
+                    hop_out(dr, k).wait_send()
         for d in order:
             fwd(d).wait_send()
 
     @pl.when(c == 0)
     def _():
         tok_d2d.wait_send()
+        down_y.wait_send()
+        down_own.wait_send()
+        down_sib.wait_send()
         cot1.wait_send()
         cot2.wait_send()
         for sel in range(2):
@@ -376,49 +459,81 @@
         for n in range(10):
             cfwd(n).wait_send()
 
-    for cp in (gcp, rcp, ycp):
+    @pl.when(c == 1)
+    def _():
+        loads[4].wait()
+
+    for cp in stores:
+        cp.wait()
+    for cp in (gcp, rcp, hcp):
         cp.wait_send()
     for k in range(1, 8):
         prompt_send(k).wait_send()
         gate_send(k).wait_send()
         far_send(k).wait_send()
-    for k in range(1, 4):
-        near_send(k).wait_send()
+    for s in range(2):
+        for k in range(1, 4):
+            near_send(s, k).wait_send()
+
+
+def deliver(*refs):
+    ins, outs, held, (in_sem, out_sem) = refs[:4], refs[4:8], refs[8:12], refs[12:]
+    reads = [pltpu.make_async_copy(ins[n], held[n], in_sem.at[n]) for n in range(4)]
+    writes = [pltpu.make_async_copy(held[n], outs[n], out_sem.at[n]) for n in range(4)]
+    for cp in reads:
+        cp.start()
+    for n in range(4):
+        reads[n].wait()
+        writes[n].start()
+    for cp in writes:
+        cp.wait()
 
 
 def shards(tokens, cotangent, master, moment, second, prompts, up_weight, down_weight):
     V, D = pltpu.VMEM, pltpu.SemaphoreType.DMA
     vmem = pl.BlockSpec(memory_space=pltpu.VMEM)
-    hbm = pl.BlockSpec(memory_space=pl.ANY)
+    hbm = pl.BlockSpec(memory_space=pltpu.HBM)
     out = jax.ShapeDtypeStruct
-    return pl.pallas_call(
+    results = pl.pallas_call(
         kernel,
         out_shape=(
             out((200, 320), f32), out((200, 320), f32), out((200, 320), f32), out((64, 80), f32),
         ),
-        in_specs=[vmem] * 2 + [hbm] * 6,
-        out_specs=[vmem] * 4,
+        in_specs=[hbm] * 8,
+        out_specs=[hbm] * 3 + [vmem],
         scratch_shapes=[
             V((200, 320), f32), V((200, 320), f32), V((200, 320), f32),
-            V((64, 5120), bf16), V((200, 5120), bf16), V((200, 5120), bf16), V((200, 5120), bf16),
+            V((64, 320), bf16), V((200, 256), bf16),
+            V((200, 320), f32), V((200, 320), f32), V((200, 320), f32),
+            V((64, 5120), bf16), V((200, 5120), bf16), V((200, 5120), bf16),
+            V((2, 200, 2560), bf16), V((200, 2560), bf16),
             V((64, 320), bf16), V((200, 256), bf16), V((32, 64, 640), bf16),
             V((2, 200, 128), bf16), V((8, 2, 2, 200, 128), bf16), V((8, 64, 640), bf16),
             V((200, 320), bf16), V((200, 320), bf16), V((200, 320), bf16), V((200, 320), bf16),
             V((200, 640), bf16),
             V((8, 64, 200), f32), V((8, 64, 200), bf16), V((8, 64, 200), bf16),
-            V((64, 2560), f32), V((64, 2560), bf16), V((64, 2560), bf16),
-            V((4, 64, 640), f32), V((4, 64, 640), bf16), V((4, 64, 640), bf16),
-            V((8, 64, 80), f32), V((8, 64, 80), bf16), V((8, 64, 80), bf16),
-            D((6,)), D((3,)), D((3,)), D((2, 8)), D((2, 8)), D((2, 8)), D((2, 8)),
+            V((64, 200), bf16), V((64, 200), bf16),
+            V((4, 64, 640), f32), V((4, 64, 640), bf16), V((3, 64, 640), bf16),
+            V((8, 40, 128), f32), V((8, 40, 128), bf16), V((7, 40, 128), bf16),
+            D((8,)), D((3,)), D((4,)), D((4,)), D((2, 16)), D((2, 16, CH)), D((2, 8)), D((2, 8)),
             D((32,)), D((32,)),
             D(()), D(()), D(()), D(()), D((2, 2)), D((2, 2)), D((2, 2)), D((2, 2)),
             D((10,)), D((10,)),
-            D((8,)), D((8,)), D((8,)), D((8,)), D(()), D(()), D((4,)), D((4,)), D((8,)), D((8,)),
+            D((8,)), D((8,)), D((8,)), D((8,)), D((3,)), D((3,)),
+            D((2, 4)), D((2, 4)), D((8,)), D((8,)),
         ],
         compiler_params=pltpu.CompilerParams(
-            collective_id=0, has_side_effects=True, vmem_limit_bytes=56 * 1024 * 1024
+            collective_id=0, has_side_effects=True, vmem_limit_bytes=65_900_000
         ),
     )(tokens, cotangent.T, master, moment, second, prompts, up_weight, down_weight)
+    return pl.pallas_call(
+        deliver,
+        out_shape=tuple(out(r.shape, f32) for r in results),
+        in_specs=[hbm] * 4,
+        out_specs=[hbm] * 4,
+        scratch_shapes=[V(r.shape, f32) for r in results] + [D((4,)), D((4,))],
+        compiler_params=pltpu.CompilerParams(vmem_limit_bytes=65_900_000),
+    )(*results)
 
 
 def solution(mesh):

time: 114 us -> 106 us (0.930)
  the two profiles are of different devices: /device:TPU:110 before, /device:TPU:48 now
where the time goes in v2:
time: 106 us
  Pallas kernels  106 us (100%)
    pallas_call x1, Pallas kernels, shards(): pl.pallas_call(kernel, out_shape=(out((200, 320), f32), out((200, 320), f...  104 us

profile of v2, /device:TPU:48, one launch (start us, length us, event | category | flops | bytes accessed | tf_op | source)
XLA Modules:
  0.0 106.3 jit_solution(2670153353987801621)
XLA Ops:
  0.6 103.7 %shard_map.111 = (f32[200,320]{1,0:T(8,128)}, f32[200,320]{1,0:T(8,128)}, f32[200,320]{1,0:T(8,128)}, f32[64,80]{1,0:T(8,128)}) custom-call(bf16[64,320]{1,0:T(8,128)(2,1)} %tok_hbm.1, bf16[200,256]{1,0:T(8,128)(2,1)} %bitcast.1, f32[200,320]{1,0:T(8,128)} %master_hbm.1, f32[200,320]{1,0:T(8,128)} %moment_hbm.1, f32[200,320]{1,0:T(8,128)} %second_hbm.1, ...), custom_call_target="tpu_custom_call" | custom-call | tf_op jit(solution)/shard_map/pallas_call | solution.py:497
  104.4 2.0 %shard_map.112 = (f32[200,320]{1,0:T(8,128)}, f32[200,320]{1,0:T(8,128)}, f32[200,320]{1,0:T(8,128)}, f32[64,80]{1,0:T(8,128)}) custom-call(f32[200,320]{1,0:T(8,128)} %get-tuple-element.8.refs_0_, f32[200,320]{1,0:T(8,128)} %get-tuple-element.9.refs_1_, f32[200,320]{1,0:T(8,128)} %get-tuple-element.10.refs_2_, f32[64,80]{1,0:T(8,128)} %get-tuple-element.11.refs_3_), custom_call_target="tpu_custom_call" | custom-call | tf_op jit(solution)/shard_map/pallas_call | solution.py:529

commit v3 on v2

--- a/solution.py
+++ b/solution.py
@@ -12,7 +12,7 @@
 ROW = ("z", "yl")
 GC = ("yh", "x", "core")
 NZ = 32
-JUMP = 2
+JUMP = 3
 CH = 4
 MESH = pl.DeviceIdType.MESH
 f32 = jnp.float32
@@ -56,7 +56,7 @@
     gsend, grecv, rsend, rrecv, rcat,
     gp32, gps, gpr, hid, hrecv, a32, asend, arecv, b32, bsend, brecv,
     loc_sem, st_sem, d2d_s, d2d_r, js, jr, hs, hr, fs, fr,
-    c1s, c1r, c2s, c2r, xs, xr, x2s, x2r, cfs, cfr,
+    c1s, c1r, xs, xr, x2s, x2r, cfs, cfr,
     ps, pr, gs, gr, ds_, dr_, as_, ar, bs, br,
 ):
     yh, z, yl, x, c = (lax.axis_index(a) for a in AXES)
@@ -98,7 +98,7 @@
 
     barrier = pltpu.get_barrier_semaphore()
     peers = [sib, yn]
-    peers += [{"z": wrap(z + d, NZ)} for d in (1, -1, 2, -2)]
+    peers += [{"z": wrap(z + d, NZ)} for d in (1, -1, JUMP, -JUMP)]
     peers += [near_peer(s, k)[1] for s in range(2) for k in range(1, 4)]
     peers += [chip_peer(k)[1] for k in range(1, 8)]
     peers += [prompt_peer(k)[1] for k in range(1, 8)]
@@ -125,7 +125,7 @@
         return remote(b, b, fs.at[order[d]], fr.at[order[d]], sib)
 
     rows = 64 // CH
-    steps = 16 // JUMP
+    steps = 5
 
     def side(dr):
         return 0 if dr > 0 else 1
@@ -145,20 +145,20 @@
         b, i = tok_all.at[block(dr * JUMP * k)], side(dr)
         return remote(b, b, js.at[i, k], jr.at[i, k, 0], {"z": wrap(z + JUMP * dr, NZ)})
 
-    def hop(dr, k, ch):
-        b, i = piece(dr * 2 * k, ch), side(dr)
-        return remote(b, b, hs.at[i, k], hr.at[i, k], {"z": wrap(z + dr, NZ)})
-
-    def hop_out(dr, k):
-        b, i = tok_all.at[block(dr * 2 * k)], side(dr)
-        return remote(b, b, hs.at[i, k], hr.at[i, k], {"z": wrap(z + dr, NZ)})
-
-    def hop_in(dr, k):
-        b, i = tok_all.at[block(dr * (2 * k + 1))], side(dr)
-        return remote(b, b, hs.at[i, k], hr.at[i, k], {"z": wrap(z + dr, NZ)})
-
-    def njump(dr):
-        return steps if dr > 0 else steps - 1
+    def hop(dr, k, way, ch):
+        b, i = piece(dr * JUMP * k, ch), 2 * side(dr) + side(way)
+        return remote(b, b, hs.at[i, k], hr.at[i, k], {"z": wrap(z + dr * way, NZ)})
+
+    def hop_out(dr, k, way):
+        b, i = tok_all.at[block(dr * JUMP * k)], 2 * side(dr) + side(way)
+        return remote(b, b, hs.at[i, k], hr.at[i, k], {"z": wrap(z + dr * way, NZ)})
+
+    def hop_in(dr, k, way):
+        b, i = tok_all.at[block(dr * (JUMP * k + way))], 2 * side(dr) + side(way)
+        return remote(b, b, hs.at[i, k], hr.at[i, k], {"z": wrap(z + dr * way, NZ)})
+
+    def ways(dr, k):
+        return [w for w in (1, -1) if (k > 0 or w > 0) and (dr > 0 or k < steps or w < 0)]
 
     def prompt_send(k):
         o, peer = prompt_peer(k)
@@ -173,52 +173,41 @@
             prompt_send(k).start()
         p_all[h] = prompts_v[:, pl.ds(pl.multiple_of(h * 640, 128), 640)]
 
-    hy = (1 - yh) * 4 + x
-
-    def hx(sel, d):
-        return (yh if sel == 0 else 1 - yh) * 4 + wrap(x + d, 4)
-
-    cot1 = remote(cs_send, cot_all.at[h, yl], c1s, c1r, yn)
-    cot1_in = remote(cs_send, cot_all.at[h, 1 - yl], c1s, c1r, yn)
-    cot2 = remote(cot_all.at[h], cot_all.at[h], c2s, c2r, {"yh": 1 - yh})
-    cot2_in = remote(cot_all.at[hy], cot_all.at[hy], c2s, c2r, {"yh": 1 - yh})
-
-    def xsend(sel, dr):
-        b = cot_all.at[hx(sel, 0)]
-        i = 0 if dr > 0 else 1
-        return remote(b, b, xs.at[i, sel], xr.at[i, sel], {"x": wrap(x + dr, 4)})
-
-    def xin(sel, dr):
-        b = cot_all.at[hx(sel, -dr)]
-        i = 0 if dr > 0 else 1
-        return remote(b, b, xs.at[i, sel], xr.at[i, sel], {"x": wrap(x + dr, 4)})
-
-    def x2send(sel, dr):
-        i = 0 if dr > 0 else 1
-        b = cot_all.at[hx(sel, -dr), i]
-        return remote(b, b, x2s.at[i, sel], x2r.at[i, sel], {"x": wrap(x + dr, 4)})
-
-    def x2in(sel, dr):
-        i = 0 if dr > 0 else 1
-        b = cot_all.at[hx(sel, -2 * dr), i]
-        return remote(b, b, x2s.at[i, sel], x2r.at[i, sel], {"x": wrap(x + dr, 4)})
-
-    def cfwd(n):
-        if n == 0:
-            b = cot_all.at[h]
-        elif n == 1:
-            b = cot_all.at[hy]
-        elif n < 6:
-            sel, i = (n - 2) // 2, (n - 2) % 2
-            b = cot_all.at[hx(sel, -1 if i == 0 else 1)]
-        else:
-            sel, i = (n - 6) // 2, (n - 6) % 2
-            b = cot_all.at[hx(sel, 2), i]
-        return remote(b, b, cfs.at[n], cfr.at[n], sib)
+    def hp(j, d):
+        return (yh if j < 2 else 1 - yh) * 4 + wrap(x + d, 4)
+
+    def lp(j):
+        return yl if j % 2 == 0 else 1 - yl
+
+    def ysend(j):
+        src = cs_send if j % 2 else cot_all.at[h, yl]
+        peer = {"yh": yh if j < 2 else 1 - yh, "yl": lp(j)}
+        return remote(src, cot_all.at[h, yl], c1s.at[j], c1r.at[j], peer)
+
+    def xsend(j, dr):
+        b, i = cot_all.at[hp(j, 0), lp(j)], side(dr)
+        return remote(b, b, xs.at[i, j], xr.at[i, j], {"x": wrap(x + dr, 4)})
+
+    def x2send(j):
+        dr = -1 if j % 2 else 1
+        b = cot_all.at[hp(j, -dr), lp(j)]
+        return remote(b, b, x2s.at[j], x2r.at[j], {"x": wrap(x + dr, 4)})
+
+    def cfwd(j, d):
+        b = cot_all.at[hp(j, d), lp(j)]
+        return remote(b, b, cfs.at[j, d], cfr.at[j, d], sib)
 
     down_y = remote(dperm.at[1 - yl], dother, ds_.at[0], dr_.at[0], yn)
     down_own = remote(dperm.at[yl], dperm.at[yl], ds_.at[1], dr_.at[1], sib)
     down_sib = remote(dother, dother, ds_.at[2], dr_.at[2], sib)
+
+    def arrange(l):
+        for zz in range(32):
+            col = 80 * (2 * zz + l)
+            at, part = zz % 4 * 640, zz // 4
+            dperm[l, :, at + 64 * part : at + 64 * part + 64] = down_v[:, col : col + 64]
+            at += 512 + 16 * part
+            dperm[l, :, at : at + 16] = down_v[:, col + 64 : col + 80]
 
     @pl.when(c == 1)
     def _():
@@ -231,29 +220,32 @@
         for ch in range(CH):
             for dr in (1, -1):
                 jump(dr, 0, ch).start()
-                if JUMP == 2:
-                    hop(dr, 0, ch).start()
+            for dr in (1, -1):
+                hop(dr, 0, 1, ch).start()
         fwd(0).start()
         for k in range(1, steps + 1):
             for ch in range(CH):
                 for dr in (1, -1):
-                    if k > njump(dr):
-                        continue
                     jump_in(dr, k - 1, ch).wait_recv()
-                    if k < njump(dr):
+                    if k < steps:
                         jump(dr, k, ch).start()
-                    if JUMP == 2 and k < steps:
-                        hop(dr, k, ch).start()
+                    for way in ways(dr, k):
+                        hop(dr, k, way, ch).start()
                     if ch == CH - 1:
                         fwd(dr * JUMP * k).start()
-            if JUMP == 2:
-                for dr in (1, -1):
-                    hop_in(dr, k - 1).wait_recv()
-                    fwd(dr * (2 * k - 1)).start()
-            if k == steps // 4:
+            if k == 2:
                 send_prompts()
-        for n in range(10):
-            cfwd(n).wait_recv()
+            for dr in (1, -1):
+                for way in ways(dr, k - 1):
+                    hop_in(dr, k - 1, way).wait_recv()
+                    fwd(dr * (JUMP * (k - 1) + way)).start()
+        for dr in (1, -1):
+            for way in ways(dr, steps):
+                hop_in(dr, steps, way).wait_recv()
+                fwd(dr * (JUMP * steps + way)).start()
+        for j in range(4):
+            for d in range(4):
+                cfwd(j, d).wait_recv()
 
     @pl.when(c == 0)
     def _():
@@ -266,34 +258,34 @@
             first = yl == 0
             cot_all[h, yl, core] = jnp.where(first, even, odd)
             cs_send[core] = jnp.where(first, odd, even)
-        cot1.start()
-        cot1_in.wait_recv()
-        cot2.start()
-        for dr in (1, -1):
-            xsend(0, dr).start()
-        cfwd(0).start()
-        cot2_in.wait_recv()
-        for dr in (1, -1):
-            xsend(1, dr).start()
-        cfwd(1).start()
-        for sel in range(2):
-            for i, dr in enumerate((1, -1)):
-                xin(sel, dr).wait_recv()
-                x2send(sel, dr).start()
-                cfwd(2 + 2 * sel + i).start()
+        for j in (1, 3, 2):
+            ysend(j).start()
+        for j in (0, 1, 3, 2):
+            if j:
+                ysend(j).wait_recv()
+            for dr in (1, -1):
+                xsend(j, dr).start()
+            cfwd(j, 0).start()
+        loads[4].wait()
+        for l in range(2):
+            @pl.when(yl != l)
+            def _():
+                arrange(l)
+        down_y.start()
+        for j in (0, 1, 3, 2):
+            for dr in (1, -1):
+                xsend(j, dr).wait_recv()
+                if dr == (-1 if j % 2 else 1):
+                    x2send(j).start()
+                cfwd(j, 1 if dr < 0 else 3).start()
         send_prompts()
-        for sel in range(2):
-            for i, dr in enumerate((1, -1)):
-                x2in(sel, dr).wait_recv()
-                cfwd(6 + 2 * sel + i).start()
-        loads[4].wait()
-        for r in range(64):
-            zz, l = r // 2, r % 2
-            at, part = zz % 4 * 640, zz // 4
-            dperm[l, :, at + 64 * part : at + 64 * part + 64] = down_v[:, 80 * r : 80 * r + 64]
-            at += 512 + 16 * part
-            dperm[l, :, at : at + 16] = down_v[:, 80 * r + 64 : 80 * r + 80]
-        down_y.start()
+        for j in (0, 1, 3, 2):
+            x2send(j).wait_recv()
+            cfwd(j, 2).start()
+        for l in range(2):
+            @pl.when(yl == l)
+            def _():
+                arrange(l)
         down_own.start()
         for d in order:
             fwd(d).wait_recv()
@@ -436,11 +428,11 @@
     def _():
         cot_d2d.wait_send()
         for dr in (1, -1):
-            for k in range(steps):
-                if k < njump(dr):
+            for k in range(steps + 1):
+                if k < steps:
                     jump_out(dr, k).wait_send()
-                if JUMP == 2:
-                    hop_out(dr, k).wait_send()
+                for way in ways(dr, k):
+                    hop_out(dr, k, way).wait_send()
         for d in order:
             fwd(d).wait_send()
 
@@ -450,14 +442,14 @@
         down_y.wait_send()
         down_own.wait_send()
         down_sib.wait_send()
-        cot1.wait_send()
-        cot2.wait_send()
-        for sel in range(2):
+        for j in range(4):
+            if j:
+                ysend(j).wait_send()
             for dr in (1, -1):
-                xsend(sel, dr).wait_send()
-                x2send(sel, dr).wait_send()
-        for n in range(10):
-            cfwd(n).wait_send()
+                xsend(j, dr).wait_send()
+            x2send(j).wait_send()
+            for d in range(4):
+                cfwd(j, d).wait_send()
 
     @pl.when(c == 1)
     def _():
@@ -515,10 +507,10 @@
             V((64, 200), bf16), V((64, 200), bf16),
             V((4, 64, 640), f32), V((4, 64, 640), bf16), V((3, 64, 640), bf16),
             V((8, 40, 128), f32), V((8, 40, 128), bf16), V((7, 40, 128), bf16),
-            D((8,)), D((3,)), D((4,)), D((4,)), D((2, 16)), D((2, 16, CH)), D((2, 8)), D((2, 8)),
+            D((8,)), D((3,)), D((4,)), D((4,)), D((2, 5)), D((2, 5, CH)), D((4, 6)), D((4, 6)),
             D((32,)), D((32,)),
-            D(()), D(()), D(()), D(()), D((2, 2)), D((2, 2)), D((2, 2)), D((2, 2)),
-            D((10,)), D((10,)),
+            D((4,)), D((4,)), D((2, 4)), D((2, 4)), D((4,)), D((4,)),
+            D((4, 4)), D((4, 4)),
             D((8,)), D((8,)), D((8,)), D((8,)), D((3,)), D((3,)),
             D((2, 4)), D((2, 4)), D((8,)), D((8,)),
         ],

time: 106 us -> 93.6 us (0.88)
  the two profiles are of different devices: /device:TPU:48 before, /device:TPU:66 now
where the time goes in v3:
time: 93.6 us; the launch traced here: 93.5 us
  Pallas kernels  92.8 us (99%)
    pallas_call x1, Pallas kernels, shards(): pl.pallas_call(kernel, out_shape=(out((200, 320), f32), out((200, 320), f...  90.9 us
    pallas_call x1, Pallas kernels, shards(): pl.pallas_call(deliver, out_shape=tuple((out(r.shape, f32) for r in resul...  1.96 us

profile of v3, /device:TPU:66, one launch (start us, length us, event | category | flops | bytes accessed | tf_op | source)
XLA Modules:
  0.0 93.5 jit_solution(11810365085064304885)
XLA Ops:
  0.6 90.9 %shard_map.111 = (f32[200,320]{1,0:T(8,128)}, f32[200,320]{1,0:T(8,128)}, f32[200,320]{1,0:T(8,128)}, f32[64,80]{1,0:T(8,128)}) custom-call(bf16[64,320]{1,0:T(8,128)(2,1)} %tok_hbm.1, bf16[200,256]{1,0:T(8,128)(2,1)} %bitcast.1, f32[200,320]{1,0:T(8,128)} %master_hbm.1, f32[200,320]{1,0:T(8,128)} %moment_hbm.1, f32[200,320]{1,0:T(8,128)} %second_hbm.1, ...), custom_call_target="tpu_custom_call" | custom-call | tf_op jit(solution)/shard_map/pallas_call | solution.py:489
  91.5 2.0 %shard_map.112 = (f32[200,320]{1,0:T(8,128)}, f32[200,320]{1,0:T(8,128)}, f32[200,320]{1,0:T(8,128)}, f32[64,80]{1,0:T(8,128)}) custom-call(f32[200,320]{1,0:T(8,128)} %get-tuple-element.8.refs_0_, f32[200,320]{1,0:T(8,128)} %get-tuple-element.9.refs_1_, f32[200,320]{1,0:T(8,128)} %get-tuple-element.10.refs_2_, f32[64,80]{1,0:T(8,128)} %get-tuple-element.11.refs_3_), custom_call_target="tpu_custom_call" | custom-call | tf_op jit(solution)/shard_map/pallas_call | solution.py:521

commit v4 on v3

--- a/solution.py
+++ b/solution.py
@@ -233,7 +233,7 @@
                         hop(dr, k, way, ch).start()
                     if ch == CH - 1:
                         fwd(dr * JUMP * k).start()
-            if k == 2:
+            if k == 4:
                 send_prompts()
             for dr in (1, -1):
                 for way in ways(dr, k - 1):
@@ -266,18 +266,18 @@
             for dr in (1, -1):
                 xsend(j, dr).start()
             cfwd(j, 0).start()
+        for j in (0, 1, 3, 2):
+            for dr in (1, -1):
+                xsend(j, dr).wait_recv()
+                if dr == (-1 if j % 2 else 1):
+                    x2send(j).start()
+                cfwd(j, 1 if dr < 0 else 3).start()
         loads[4].wait()
         for l in range(2):
             @pl.when(yl != l)
             def _():
                 arrange(l)
         down_y.start()
-        for j in (0, 1, 3, 2):
-            for dr in (1, -1):
-                xsend(j, dr).wait_recv()
-                if dr == (-1 if j % 2 else 1):
-                    x2send(j).start()
-                cfwd(j, 1 if dr < 0 else 3).start()
         send_prompts()
         for j in (0, 1, 3, 2):
             x2send(j).wait_recv()
@@ -340,10 +340,9 @@
     rcat[:, :320] = jnp.where(first_core, mine, other)
     rcat[:, 320:] = jnp.where(first_core, other, mine)
 
-    for o in range(8):
-        v = nt(p_all[o], rcat[...])
-        gp32[o] = v
-        gps[o] = v.astype(bf16)
+    v = nt(p_all[...].reshape(512, 640), rcat[...]).reshape(8, 64, 200)
+    gps[...] = v.astype(bf16)
+    gp32[...] = v
 
     def gate_send(k):
         o, peer = chip_peer(k)
@@ -377,13 +376,15 @@
         part = pl.ds(32 * s, 32)
         return remote(asend.at[o, part], arecv.at[k - 1, part], as_.at[s, k], ar.at[s, k], peer)
 
-    for o in range(4):
-        v = a32[o] + nn(hidden, dother[:, 640 * o : 640 * o + 640])
-        a32[o] = v
-        asend[o] = v.astype(bf16)
-    for s in range(2):
-        for k in (2, 1, 3):
-            near_send(s, k).start()
+    for k in (2, 1, 3, 0):
+        o = lax.rem(zl + k, 4)
+        v = a32[o] + nn(hidden, dother[:, pl.ds(pl.multiple_of(640 * o, 128), 640)])
+        if k == 0:
+            a32[o] = v
+        else:
+            asend[o] = v.astype(bf16)
+            for s in range(2):
+                near_send(s, k).start()
 
     def far_send(k):
         o = lax.rem(zh + k, 8)

time: 93.6 us -> 91.9 us (0.982)
  the two profiles are of different devices: /device:TPU:66 before, /device:TPU:96 now
where the time goes in v4:
time: 91.9 us; the launch traced here: 91.7 us
  Pallas kernels  91.1 us (99%)
    pallas_call x1, Pallas kernels, shards(): pl.pallas_call(kernel, out_shape=(out((200, 320), f32), out((200, 320), f...  89.1 us
    pallas_call x1, Pallas kernels, shards(): pl.pallas_call(deliver, out_shape=tuple((out(r.shape, f32) for r in resul...  1.96 us

profile of v4, /device:TPU:96, one launch (start us, length us, event | category | flops | bytes accessed | tf_op | source)
XLA Modules:
  0.0 91.7 jit_solution(9511613786448357415)
XLA Ops:
  0.6 89.1 %shard_map.111 = (f32[200,320]{1,0:T(8,128)}, f32[200,320]{1,0:T(8,128)}, f32[200,320]{1,0:T(8,128)}, f32[64,80]{1,0:T(8,128)}) custom-call(bf16[64,320]{1,0:T(8,128)(2,1)} %tok_hbm.1, bf16[200,256]{1,0:T(8,128)(2,1)} %bitcast.1, f32[200,320]{1,0:T(8,128)} %master_hbm.1, f32[200,320]{1,0:T(8,128)} %moment_hbm.1, f32[200,320]{1,0:T(8,128)} %second_hbm.1, ...), custom_call_target="tpu_custom_call" | custom-call | tf_op jit(solution)/shard_map/pallas_call | solution.py:490
  89.8 2.0 %shard_map.112 = (f32[200,320]{1,0:T(8,128)}, f32[200,320]{1,0:T(8,128)}, f32[200,320]{1,0:T(8,128)}, f32[64,80]{1,0:T(8,128)}) custom-call(f32[200,320]{1,0:T(8,128)} %get-tuple-element.8.refs_0_, f32[200,320]{1,0:T(8,128)} %get-tuple-element.9.refs_1_, f32[200,320]{1,0:T(8,128)} %get-tuple-element.10.refs_2_, f32[64,80]{1,0:T(8,128)} %get-tuple-element.11.refs_3_), custom_call_target="tpu_custom_call" | custom-call | tf_op jit(solution)/shard_map/pallas_call | solution.py:522
